TPU v7x, 32 devices: a whole 2x2x4 slice. The times are simulated.
32 devices in a mesh: gx: 16 (over z, y, x), gy: 1, gz: 2 (over core).
Axes of the slice: x: 2, y: 2, z: 4, core: 2. Of those that a mesh axis runs over, the one named last changes fastest.
Arguments:
- populations: float32 [19, 128, 8, 256], P(None, 'gx', 'gy', 'gz'), may hold values from 0.01 to 0.11
Outputs:
- populations_next: float32 [19, 128, 8, 256], P(None, 'gx', 'gy', 'gz')
- moments_slab: float32 [4, 256, 8, 128], P(None, ('gz', 'gx'), 'gy')
All inputs are finite; a program needn't handle non-finite values.
Results may differ from a plain program's by a relative error of at most 0.0003.
Values sent between devices are 32-bit elements; how exact they have to be, the bound alone decides.
A program may use at most 64 MiB of HBM per device.

v0:
```python
import functools

import jax
import jax.numpy as jnp
from jax import lax
from jax.experimental import pallas as pl
from jax.experimental.pallas import tpu as pltpu
from jax.sharding import PartitionSpec as P

MESH = pl.DeviceIdType.MESH

lattice_moves = [
    (0, 0, 0),
    (1, 0, 0),
    (-1, 0, 0),
    (0, 1, 0),
    (0, -1, 0),
    (0, 0, 1),
    (0, 0, -1),
    (1, 1, 0),
    (-1, -1, 0),
    (1, -1, 0),
    (-1, 1, 0),
    (1, 0, 1),
    (-1, 0, -1),
    (1, 0, -1),
    (-1, 0, 1),
    (0, 1, 1),
    (0, -1, -1),
    (0, 1, -1),
    (0, -1, 1),
]
lattice_weights = [1.0 / 3.0] + [1.0 / 18.0] * 6 + [1.0 / 36.0] * 12
relaxation = 1.6
count_q = len(lattice_moves)


def movers(component, sign):
    return [q for q, move in enumerate(lattice_moves) if move[component] == sign]


def place_in(q, component):
    return movers(component, lattice_moves[q][component]).index(q)


def side(sign):
    return 0 if sign > 0 else 1


edges_xz = [q for q, m in enumerate(lattice_moves) if m[0] and m[2]]
edges_xy = [q for q, m in enumerate(lattice_moves) if m[0] and m[1]]
edges_yz = [q for q, m in enumerate(lattice_moves) if m[1] and m[2]]


def total(terms):
    terms = list(terms)
    while len(terms) > 1:
        terms = [
            terms[i] + terms[i + 1] if i + 1 < len(terms) else terms[i]
            for i in range(0, len(terms), 2)
        ]
    return terms[0]


def moments_of(f):
    density = total(f)
    inverse = 1.0 / density
    velocity = []
    for component in range(3):
        plus = total(f[q] for q in movers(component, 1))
        minus = total(f[q] for q in movers(component, -1))
        velocity.append((plus - minus) * inverse)
    return density, velocity


def collided(f):
    density, velocity = moments_of(f)
    speed_sq = velocity[0] * velocity[0] + velocity[1] * velocity[1] + velocity[2] * velocity[2]
    base = 1.0 - 1.5 * speed_sq
    scaled = {w: (relaxation * w) * density for w in set(lattice_weights)}
    keep = 1.0 - relaxation
    result = [None] * count_q
    result[0] = keep * f[0] + scaled[lattice_weights[0]] * base
    for q in range(1, count_q, 2):
        move = lattice_moves[q]
        projected = None
        for component in range(3):
            if move[component] == 0:
                continue
            if projected is None:
                projected = velocity[component] if move[component] > 0 else -velocity[component]
            elif move[component] > 0:
                projected = projected + velocity[component]
            else:
                projected = projected - velocity[component]
        even = base + 4.5 * (projected * projected)
        odd = 3.0 * projected
        weight = scaled[lattice_weights[q]]
        result[q] = keep * f[q] + weight * (even + odd)
        result[q + 1] = keep * f[q + 1] + weight * (even - odd)
    return result


def rolled(v, shift, axis):
    return pltpu.roll(v, shift % v.shape[axis], axis)


def paired(at, k, n):
    if n & (n - 1):
        return lax.rem(at + k, n)
    bit = 1
    while bit < n:
        if k & bit:
            at = at + bit - 2 * bit * lax.rem(at // bit, 2)
        bit *= 2
    return at


def kernel(axes, sizes, pop_hbm, out_vm, slab_vm,
           pop, face_x, edge_xz, pack_x, pack_z, face_z, send_m, recv_m, mid,
           row_y, face_y, edge_xy, edge_yz,
           load_sem, send_sem, recv_sem, send_m_sem, recv_m_sem):
    nx, ny, nz = (sizes[a] for a in axes)
    here = tuple(lax.axis_index(a) for a in axes)
    _, lx, ly, lz = pop.shape
    split_y = ny > 1

    def device_at(offset):
        return tuple(
            lax.rem(h + (o % n), n) if o % n else h
            for h, o, n in zip(here, offset, (nx, ny, nz))
        )

    offsets = [(k, 0, 0) for k in range(1, nx)]
    offsets += [(0, 0, 1), (0, 0, -1)]
    offsets += [lattice_moves[q] for q in edges_xz]
    if split_y:
        offsets += [(0, 1, 0), (0, -1, 0)]
        offsets += [lattice_moves[q] for q in edges_xy + edges_yz]
    partners = sorted({(a % nx, b % ny, c % nz) for a, b, c in offsets})
    barrier = pltpu.get_barrier_semaphore()
    for offset in partners:
        pl.semaphore_signal(barrier, inc=1, device_id=device_at(offset), device_id_type=MESH)

    load = pltpu.make_async_copy(pop_hbm, pop, load_sem)
    load.start()
    load.wait()

    lane = lax.broadcasted_iota(jnp.int32, (ly, lz), 1)
    row = lax.broadcasted_iota(jnp.int32, (ly, lz), 0)

    for sign in (1, -1):
        at = lz - 1 if sign > 0 else 0
        packed = jnp.zeros((ly, lz), jnp.float32)
        for i, q in enumerate(movers(2, sign)):
            for x in range(lx):
                k = i * lx + x
                packed = jnp.where(lane == k, rolled(pop[q, x], k - at, 1), packed)
        pack_z[side(sign)] = packed
    for sign in (1, -1):
        at = lx - 1 if sign > 0 else 0
        up, down = (lattice_moves.index((sign, 0, cz)) for cz in (1, -1))
        pack_x[side(sign)] = jnp.where(lane == lz - 1, pop[up, at], pop[down, at])
    if split_y:
        for sign in (1, -1):
            at = ly - 1 if sign > 0 else 0
            for i, q in enumerate(movers(1, sign)):
                for x in range(lx):
                    row_y[side(sign), i, x:x + 1, :] = pop[q, x, at:at + 1, :]

    values = [[None] * lx for _ in range(4)]
    for x in range(lx):
        density, velocity = moments_of([pop[q, x] for q in range(count_q)])
        for c, v in enumerate([density] + velocity):
            values[c][x] = v
    for c in range(4):
        tiles = values[c]
        step = 1
        while step < lx:
            upper = (lane & step) != 0
            fresh = list(tiles)
            for x in range(lx):
                if x & step:
                    continue
                a, b = tiles[x], tiles[x + step]
                fresh[x] = jnp.where(upper, rolled(b, step, 1), a)
                fresh[x + step] = jnp.where(upper, b, rolled(a, -step, 1))
            tiles = fresh
            step *= 2
        for z in range(lx):
            mid[c, z * ly:(z + 1) * ly, :] = tiles[z]
    for p in range(2):
        square = mid[2 * p:2 * p + 2].reshape(lz, lz).T
        for j in range(nx):
            send_m[j, p] = square[j * lx:(j + 1) * lx]

    pl.semaphore_wait(barrier, len(partners))

    me = here[0]
    outgoing = []
    count = [0]

    def send(src, dst, offset):
        s = count[0]
        count[0] += 1
        copy = pltpu.make_async_remote_copy(
            src_ref=src, dst_ref=dst, send_sem=send_sem.at[s], recv_sem=recv_sem.at[s],
            device_id=device_at(offset), device_id_type=MESH)
        copy.start()
        outgoing.append(copy)
        return copy

    moment_copies = []

    def send_moments(k):
        target = (paired(here[0], k, nx),) + here[1:]
        copy = pltpu.make_async_remote_copy(
            src_ref=send_m.at[target[0]], dst_ref=recv_m.at[me],
            send_sem=send_m_sem.at[k], recv_sem=recv_m_sem.at[k],
            device_id=target, device_id_type=MESH)
        copy.start()
        moment_copies.append(copy)

    z_copies, x_copies = [], []
    for sign in (1, -1):
        s = side(sign)
        z_copies.append(send(pack_z.at[s], face_z.at[s], (0, 0, sign)))
    for sign in (1, -1):
        s, at = side(sign), lx - 1 if sign > 0 else 0
        for i, q in enumerate(movers(0, sign)):
            x_copies.append(send(pop.at[q, at], face_x.at[s, i], (sign, 0, 0)))
    edge_slot = {}
    for i, q in enumerate(edges_xz):
        cx, _, cz = lattice_moves[q]
        if (cx, cz % nz) not in edge_slot:
            edge_slot[cx, cz % nz] = i
            x_copies.append(send(pack_x.at[side(cx)], edge_xz.at[i], lattice_moves[q]))
    if split_y:
        for sign in (1, -1):
            s = side(sign)
            z_copies.append(send(row_y.at[s], face_y.at[s], (0, sign, 0)))
        for i, q in enumerate(edges_yz):
            s = side(lattice_moves[q][2])
            z_copies.append(send(pack_z.at[s], edge_yz.at[i], lattice_moves[q]))
        for i, q in enumerate(edges_xy):
            s = side(lattice_moves[q][1])
            x_copies.append(send(row_y.at[s, place_in(q, 1)], edge_xy.at[i], lattice_moves[q]))
    order = sorted(range(1, nx), key=lambda k: (k % 2 == 0, -bin(k).count("1"), abs(k - 11)))
    early = [k for k in order if bin(k).count("1") > 2]
    order = early + [k for k in order if k not in early]
    for k in early:
        send_moments(k)
    for k in order[len(early):]:
        send_moments(k)
    recv_m[me] = send_m[me]

    def streamed(q, x):
        cx, cy, cz = lattice_moves[q]
        sx = x - cx
        inside = 0 <= sx < lx
        sx_wrapped = sx % lx
        v = pop[q, sx] if inside else face_x[side(cx), place_in(q, 0)]
        if cy and split_y:
            at = ly - 1 if cy > 0 else 0
            if inside:
                other = face_y[side(cy), place_in(q, 1), sx:sx + 1, :]
            else:
                other = edge_xy[edges_xy.index(q), sx_wrapped:sx_wrapped + 1, :]
            v = jnp.where(row == at, jnp.broadcast_to(other, v.shape), v)
        if cz:
            at = lz - 1 if cz > 0 else 0
            if inside:
                other = face_z[side(cz)]
                if cy and split_y:
                    at_y = ly - 1 if cy > 0 else 0
                    other = jnp.where(row == at_y, edge_yz[edges_yz.index(q)], other)
                k = place_in(q, 2) * lx + sx
                other = rolled(other, at - k, 1)
            else:
                other = edge_xz[edge_slot[cx, cz % nz]]
            v = jnp.where(lane == at, other, v)
        if cy:
            v = rolled(v, cy, 0)
        if cz:
            v = rolled(v, cz, 1)
        return v

    def advance(x):
        result = collided([streamed(q, x) for q in range(count_q)])
        for q in range(count_q):
            out_vm[q, x] = result[q]

    for copy in z_copies:
        copy.wait_recv()
    for x in range(1, lx - 1):
        advance(x)
    for copy in x_copies:
        copy.wait_recv()
    advance(0)
    advance(lx - 1)

    for copy in moment_copies:
        copy.wait_recv()
    for p in range(2):
        square = recv_m[:, p].reshape(lz, lz).T
        slab_vm[2 * p:2 * p + 2] = square.reshape(2, lx, ly, lz)
    for copy in outgoing + moment_copies:
        copy.wait_send()


def write_out(next_vm, slab_vm, next_ref, slab_ref, sems):
    stores = [
        pltpu.make_async_copy(next_vm, next_ref, sems.at[0]),
        pltpu.make_async_copy(slab_vm, slab_ref, sems.at[1]),
    ]
    for store in stores:
        store.start()
    for store in stores:
        store.wait()


def on_device(axes, sizes, populations):
    q, lx, ly, lz = populations.shape
    nx = sizes[axes[0]]
    messages = 2 + 10 + 4
    if sizes[axes[1]] > 1:
        messages += 2 + 4 + 4
    f32 = jnp.float32
    tile = (ly, lz)
    held = pl.pallas_call(
        functools.partial(kernel, axes, sizes),
        out_shape=(
            pltpu.VMEM(populations.shape, f32),
            pltpu.VMEM((4, lz // nx, ly, lx * nx), f32),
        ),
        in_specs=[pl.BlockSpec(memory_space=pl.ANY)],
        out_specs=(pl.BlockSpec(memory_space=pltpu.VMEM),) * 2,
        scratch_shapes=[
            pltpu.VMEM(populations.shape, f32),
            pltpu.VMEM((2, 5) + tile, f32),
            pltpu.VMEM((4,) + tile, f32),
            pltpu.VMEM((2,) + tile, f32),
            pltpu.VMEM((2,) + tile, f32),
            pltpu.VMEM((2,) + tile, f32),
            pltpu.VMEM((nx, 2, lx, lz), f32),
            pltpu.VMEM((nx, 2, lx, lz), f32),
            pltpu.VMEM((4, lx * ly, lz), f32),
            pltpu.VMEM((2, 5, lx, lz), f32),
            pltpu.VMEM((2, 5, lx, lz), f32),
            pltpu.VMEM((4, lx, lz), f32),
            pltpu.VMEM((4,) + tile, f32),
            pltpu.SemaphoreType.DMA,
            pltpu.SemaphoreType.DMA((messages,)),
            pltpu.SemaphoreType.DMA((messages,)),
            pltpu.SemaphoreType.DMA((nx,)),
            pltpu.SemaphoreType.DMA((nx,)),
        ],
        compiler_params=pltpu.CompilerParams(collective_id=0, has_side_effects=True),
        name="lattice_step",
    )(populations)
    held = [pltpu.with_memory_space_constraint(h, pltpu.VMEM) for h in held]
    return pl.pallas_call(
        write_out,
        out_shape=tuple(jax.ShapeDtypeStruct(h.shape, f32) for h in held),
        in_specs=[pl.BlockSpec(memory_space=pltpu.VMEM)] * 2,
        out_specs=(pl.BlockSpec(memory_space=pl.ANY),) * 2,
        scratch_shapes=[pltpu.SemaphoreType.DMA((2,))],
        name="write_out",
    )(*held)


def solution(mesh):
    axes = tuple(mesh.axis_names)
    sizes = dict(mesh.shape)
    return jax.shard_map(
        functools.partial(on_device, axes, sizes),
        mesh=mesh,
        in_specs=(P(None, "gx", "gy", "gz"),),
        out_specs=(P(None, "gx", "gy", "gz"), P(None, ("gz", "gx"), "gy", None)),
        check_vma=False,
    )
```

profile of v0, /device:TPU:0, one launch (start us, length us, event | category | flops | bytes accessed | tf_op | source)
XLA Modules:
  0.0 13.6 jit_solution(835407719020096488)
XLA Ops:
  0.6 12.1 %lattice_step.1 = (f32[19,8,8,128]{3,2,1,0:T(8,128)S(1)}, f32[4,8,8,128]{3,2,1,0:T(8,128)S(1)}) custom-call(f32[19,8,8,128]{3,2,1,0:T(8,128)} %pop_hbm.1), custom_call_target="tpu_custom_call" | custom-call | tf_op jit(solution)/shard_map/lattice_step/pallas_call | solution.py:330
  12.7 0.9 %write_out.1 = (f32[19,8,8,128]{3,2,1,0:T(8,128)}, f32[4,8,8,128]{3,2,1,0:T(8,128)}) custom-call(f32[19,8,8,128]{3,2,1,0:T(8,128)S(1)} %get-tuple-element.4.next_vm, f32[4,8,8,128]{3,2,1,0:T(8,128)S(1)} %get-tuple-element.5.slab_vm), custom_call_target="tpu_custom_call" | custom-call | tf_op jit(solution)/shard_map/write_out/pallas_call | solution.py:362
where the time goes:
time: 13.8 us; the launch traced here: 13.6 us
  Pallas kernels  13 us (94%)
  between operations  0.64 us (5%)
    pallas_call x1, Pallas kernels, on_device(): pl.pallas_call(functools.partial(kernel, axes, sizes), out_shape=(pltpu.V...  12.1 us
    pallas_call x1, Pallas kernels, on_device(): pl.pallas_call(write_out, out_shape=tuple((jax.ShapeDtypeStruct(h.shape,...  0.88 us

commit v1 on v0

v1 whole, which is shorter than its diff:
```python
import functools

import jax
import jax.numpy as jnp
from jax import lax
from jax.experimental import pallas as pl
from jax.experimental.pallas import tpu as pltpu
from jax.sharding import PartitionSpec as P

MESH = pl.DeviceIdType.MESH

lattice_moves = [
    (0, 0, 0),
    (1, 0, 0),
    (-1, 0, 0),
    (0, 1, 0),
    (0, -1, 0),
    (0, 0, 1),
    (0, 0, -1),
    (1, 1, 0),
    (-1, -1, 0),
    (1, -1, 0),
    (-1, 1, 0),
    (1, 0, 1),
    (-1, 0, -1),
    (1, 0, -1),
    (-1, 0, 1),
    (0, 1, 1),
    (0, -1, -1),
    (0, 1, -1),
    (0, -1, 1),
]
lattice_weights = [1.0 / 3.0] + [1.0 / 18.0] * 6 + [1.0 / 36.0] * 12
relaxation = 1.6
count_q = len(lattice_moves)


def movers(component, sign):
    return [q for q, move in enumerate(lattice_moves) if move[component] == sign]


def place_in(q, component):
    return movers(component, lattice_moves[q][component]).index(q)


def side(sign):
    return 0 if sign > 0 else 1


edges_xz = [q for q, m in enumerate(lattice_moves) if m[0] and m[2]]
edges_xy = [q for q, m in enumerate(lattice_moves) if m[0] and m[1]]
edges_yz = [q for q, m in enumerate(lattice_moves) if m[1] and m[2]]


def total(terms):
    terms = list(terms)
    while len(terms) > 1:
        terms = [
            terms[i] + terms[i + 1] if i + 1 < len(terms) else terms[i]
            for i in range(0, len(terms), 2)
        ]
    return terms[0]


def moments_of(f):
    density = total(f)
    inverse = 1.0 / density
    velocity = []
    for component in range(3):
        plus = total(f[q] for q in movers(component, 1))
        minus = total(f[q] for q in movers(component, -1))
        velocity.append((plus - minus) * inverse)
    return density, velocity


def collided(f):
    density, velocity = moments_of(f)
    speed_sq = velocity[0] * velocity[0] + velocity[1] * velocity[1] + velocity[2] * velocity[2]
    base = 1.0 - 1.5 * speed_sq
    scaled = {w: (relaxation * w) * density for w in set(lattice_weights)}
    keep = 1.0 - relaxation
    result = [None] * count_q
    result[0] = keep * f[0] + scaled[lattice_weights[0]] * base
    for q in range(1, count_q, 2):
        move = lattice_moves[q]
        projected = None
        for component in range(3):
            if move[component] == 0:
                continue
            if projected is None:
                projected = velocity[component] if move[component] > 0 else -velocity[component]
            elif move[component] > 0:
                projected = projected + velocity[component]
            else:
                projected = projected - velocity[component]
        even = base + 4.5 * (projected * projected)
        odd = 3.0 * projected
        weight = scaled[lattice_weights[q]]
        result[q] = keep * f[q] + weight * (even + odd)
        result[q + 1] = keep * f[q + 1] + weight * (even - odd)
    return result


def rolled(v, shift, axis):
    return pltpu.roll(v, shift % v.shape[axis], axis)


load_chunks = ((0, 4), (4, 8))


def kernel(axes, sizes, pop_hbm, out_vm, recv_m,
           pop, land_x, face_z, pack_x, pack_z, send_m,
           row_y, face_y, edge_xy, edge_yz,
           load_sem, send_sem, recv_sem, *y_sems):
    nx, ny, nz = (sizes[a] for a in axes)
    here = tuple(lax.axis_index(a) for a in axes)
    _, lx, ly, lz = pop.shape
    split_y = ny > 1
    faces = 2 * len(movers(0, 1))

    def device_at(offset):
        return tuple(
            lax.rem(h + o % n, n) if o % n else h
            for h, o, n in zip(here, offset, (nx, ny, nz))
        )

    loads = []
    for i, (first, last) in enumerate(load_chunks):
        planes = pl.ds(first * lx // 8, (last - first) * lx // 8)
        load = pltpu.make_async_copy(pop_hbm.at[:, planes], pop.at[:, planes], load_sem.at[i])
        load.start()
        loads.append(load)

    offsets = [(k, 0, 0) for k in range(1, nx)]
    offsets += [(0, 0, 1), (0, 0, -1)]
    offsets += [lattice_moves[q] for q in edges_xz]
    if split_y:
        offsets += [(0, 1, 0), (0, -1, 0)]
        offsets += [lattice_moves[q] for q in edges_xy + edges_yz]
    partners = sorted({(a % nx, b % ny, c % nz) for a, b, c in offsets})
    barrier = pltpu.get_barrier_semaphore()
    for offset in partners:
        pl.semaphore_signal(barrier, inc=1, device_id=device_at(offset), device_id_type=MESH)

    lane = lax.broadcasted_iota(jnp.int32, (ly, lz), 1)
    row = lax.broadcasted_iota(jnp.int32, (ly, lz), 0)

    def remote(src, dst, sem, offset):
        return pltpu.make_async_remote_copy(
            src_ref=src, dst_ref=dst, send_sem=send_sem.at[sem], recv_sem=recv_sem.at[sem],
            device_id=device_at(offset), device_id_type=MESH)

    y_copies = []

    def send_y(src, dst, offset):
        s = len(y_copies)
        copy = pltpu.make_async_remote_copy(
            src_ref=src, dst_ref=dst, send_sem=y_sems[0].at[s], recv_sem=y_sems[1].at[s],
            device_id=device_at(offset), device_id_type=MESH)
        copy.start()
        y_copies.append(copy)

    lane_x = lane & (lx - 1)
    turned = [[None] * lx for _ in range(4)]

    def measure(x):
        density, velocity = moments_of([pop[q, x] for q in range(count_q)])
        for c, value in enumerate([density] + velocity):
            for z in range(lx):
                moved = rolled(value, x - z, 1) if x != z else value
                turned[c][z] = moved if turned[c][z] is None else jnp.where(lane_x == x, moved, turned[c][z])

    for i, (first, last) in enumerate(load_chunks):
        loads[i].wait()
        if i == len(load_chunks) - 1:
            for sign in (1, -1):
                at = lx - 1 if sign > 0 else 0
                up, down = (lattice_moves.index((sign, 0, cz)) for cz in (1, -1))
                pack_x[side(sign)] = jnp.where(lane == lz - 1, pop[up, at], pop[down, at])
            pl.semaphore_wait(barrier, len(partners))
            for sign in (1, -1):
                s, at = side(sign), lx - 1 if sign > 0 else 0
                for j, q in enumerate(movers(0, sign)):
                    remote(pop.at[q, at], land_x.at[s * faces // 2 + j], 0, (sign, 0, 0)).start()
            edge_slot = {}
            for q in edges_xz:
                cx, _, cz = lattice_moves[q]
                if (cx, cz % nz) not in edge_slot:
                    edge_slot[cx, cz % nz] = faces + len(edge_slot)
                    remote(pack_x.at[side(cx)], land_x.at[edge_slot[cx, cz % nz]], 0, lattice_moves[q]).start()
        for x in range(first * lx // 8, last * lx // 8):
            measure(x)

    for p in range(2):
        square = jnp.concatenate(turned[2 * p] + turned[2 * p + 1], axis=0).T
        for j in range(nx):
            send_m[j, p] = square[j * lx:(j + 1) * lx]

    me = here[0]
    for k in range(1, nx):
        target = lax.rem(me + k, nx)
        remote(send_m.at[target], recv_m.at[me], 2, (k, 0, 0)).start()

    for sign in (1, -1):
        at = lz - 1 if sign > 0 else 0
        packed = jnp.zeros((ly, lz), jnp.float32)
        for i, q in enumerate(movers(2, sign)):
            for x in range(lx):
                k = i * lx + x
                packed = jnp.where(lane == k, rolled(pop[q, x], k - at, 1), packed)
        pack_z[side(sign)] = packed
    for sign in (1, -1):
        s = side(sign)
        remote(pack_z.at[s], face_z.at[s], 1, (0, 0, sign)).start()
    if split_y:
        for sign in (1, -1):
            at = ly - 1 if sign > 0 else 0
            for i, q in enumerate(movers(1, sign)):
                for x in range(lx):
                    row_y[side(sign), i, x:x + 1, :] = pop[q, x, at:at + 1, :]
        for sign in (1, -1):
            s = side(sign)
            send_y(row_y.at[s], face_y.at[s], (0, sign, 0))
        for i, q in enumerate(edges_yz):
            s = side(lattice_moves[q][2])
            send_y(pack_z.at[s], edge_yz.at[i], lattice_moves[q])
        for i, q in enumerate(edges_xy):
            s = side(lattice_moves[q][1])
            send_y(row_y.at[s, place_in(q, 1)], edge_xy.at[i], lattice_moves[q])
    recv_m[me] = send_m[me]

    all_x = remote(land_x, land_x, 0, (1, 0, 0))
    all_z = remote(face_z, face_z, 1, (0, 0, 1))
    others = pl.ds(0, nx - 1)
    all_m = remote(send_m.at[others], send_m.at[others], 2, (1, 0, 0))

    def streamed(q, x):
        cx, cy, cz = lattice_moves[q]
        sx = x - cx
        inside = 0 <= sx < lx
        sx_wrapped = sx % lx
        v = pop[q, sx] if inside else land_x[side(cx) * faces // 2 + place_in(q, 0)]
        if cy and split_y:
            at = ly - 1 if cy > 0 else 0
            if inside:
                other = face_y[side(cy), place_in(q, 1), sx:sx + 1, :]
            else:
                other = edge_xy[edges_xy.index(q), sx_wrapped:sx_wrapped + 1, :]
            v = jnp.where(row == at, jnp.broadcast_to(other, v.shape), v)
        if cz:
            at = lz - 1 if cz > 0 else 0
            if inside:
                other = face_z[side(cz)]
                if cy and split_y:
                    at_y = ly - 1 if cy > 0 else 0
                    other = jnp.where(row == at_y, edge_yz[edges_yz.index(q)], other)
                k = place_in(q, 2) * lx + sx
                other = rolled(other, at - k, 1)
            else:
                other = land_x[edge_slot[cx, cz % nz]]
            v = jnp.where(lane == at, other, v)
        if cy:
            v = rolled(v, cy, 0)
        if cz:
            v = rolled(v, cz, 1)
        return v

    def advance(x):
        result = collided([streamed(q, x) for q in range(count_q)])
        for q in range(count_q):
            out_vm[q, x] = result[q]

    all_z.wait_recv()
    for copy in y_copies:
        copy.wait_recv()
    for x in range(1, lx - 1):
        advance(x)
    all_x.wait_recv()
    advance(0)
    advance(lx - 1)

    for copy in [all_x, all_z, all_m] + y_copies:
        copy.wait_send()
    all_m.wait_recv()


def finish(next_vm, recv_m, next_ref, slab_ref, slab_vm, sems):
    store = pltpu.make_async_copy(next_vm, next_ref, sems.at[0])
    store.start()
    _, lx, ly, lz = slab_vm.shape
    for p in range(2):
        square = recv_m[:, p].reshape(lz, lz).T
        slab_vm[2 * p:2 * p + 2] = square.reshape(2, lx, ly, lz)
    slab_store = pltpu.make_async_copy(slab_vm, slab_ref, sems.at[1])
    slab_store.start()
    store.wait()
    slab_store.wait()


def on_device(axes, sizes, populations):
    q, lx, ly, lz = populations.shape
    nx, ny, nz = (sizes[a] for a in axes)
    faces = 2 * len(movers(0, 1))
    edges = 4 if nz > 2 else 2
    f32 = jnp.float32
    tile = (ly, lz)
    y_sems = [pltpu.SemaphoreType.DMA((10,))] * 2 if ny > 1 else []
    held = pl.pallas_call(
        functools.partial(kernel, axes, sizes),
        out_shape=(
            pltpu.VMEM(populations.shape, f32),
            pltpu.VMEM((nx, 2, lx, lz), f32),
        ),
        in_specs=[pl.BlockSpec(memory_space=pl.ANY)],
        out_specs=(pl.BlockSpec(memory_space=pltpu.VMEM),) * 2,
        scratch_shapes=[
            pltpu.VMEM(populations.shape, f32),
            pltpu.VMEM((faces + edges,) + tile, f32),
            pltpu.VMEM((2,) + tile, f32),
            pltpu.VMEM((2,) + tile, f32),
            pltpu.VMEM((2,) + tile, f32),
            pltpu.VMEM((nx, 2, lx, lz), f32),
            pltpu.VMEM((2, 5, lx, lz), f32),
            pltpu.VMEM((2, 5, lx, lz), f32),
            pltpu.VMEM((4, lx, lz), f32),
            pltpu.VMEM((4,) + tile, f32),
            pltpu.SemaphoreType.DMA((len(load_chunks),)),
            pltpu.SemaphoreType.DMA((3,)),
            pltpu.SemaphoreType.DMA((3,)),
        ] + y_sems,
        compiler_params=pltpu.CompilerParams(collective_id=0, has_side_effects=True),
        name="lattice_step",
    )(populations)
    held = [pltpu.with_memory_space_constraint(h, pltpu.VMEM) for h in held]
    slab = (4, lx, ly, lz)
    return pl.pallas_call(
        finish,
        out_shape=(jax.ShapeDtypeStruct(populations.shape, f32), jax.ShapeDtypeStruct(slab, f32)),
        in_specs=[pl.BlockSpec(memory_space=pltpu.VMEM)] * 2,
        out_specs=(pl.BlockSpec(memory_space=pl.ANY),) * 2,
        scratch_shapes=[pltpu.VMEM(slab, f32), pltpu.SemaphoreType.DMA((2,))],
        name="finish",
    )(*held)


def solution(mesh):
    axes = tuple(mesh.axis_names)
    sizes = dict(mesh.shape)
    return jax.shard_map(
        functools.partial(on_device, axes, sizes),
        mesh=mesh,
        in_specs=(P(None, "gx", "gy", "gz"),),
        out_specs=(P(None, "gx", "gy", "gz"), P(None, ("gz", "gx"), "gy", None)),
        check_vma=False,
    )
```

time: 13.8 us -> 12.5 us (0.906)
  Pallas kernels: 13 us -> 11.7 us
    pallas_call x1, Pallas kernels: 12.1 us -> 10.8 us  [on_device(): pl.pallas_call(functools.partial(kernel, axes, sizes), out_shape=(pltpu.V...]
where the time goes in v1:
time: 12.5 us; the launch traced here: 12.3 us
  Pallas kernels  11.7 us (94%)
  between operations  0.64 us (5%)
    pallas_call x1, Pallas kernels, on_device(): pl.pallas_call(functools.partial(kernel, axes, sizes), out_shape=(pltpu.V...  10.8 us
    pallas_call x1, Pallas kernels, on_device(): pl.pallas_call(finish, out_shape=(jax.ShapeDtypeStruct(populations.shape,...  0.88 us

profile of v1, /device:TPU:0, one launch (start us, length us, event | category | flops | bytes accessed | tf_op | source)
XLA Modules:
  0.0 12.3 jit_solution(12028163406216829987)
XLA Ops:
  0.6 10.8 %lattice_step.1 = (f32[19,8,8,128]{3,2,1,0:T(8,128)S(1)}, f32[16,2,8,128]{3,2,1,0:T(8,128)S(1)}) custom-call(f32[19,8,8,128]{3,2,1,0:T(8,128)} %pop_hbm.1), custom_call_target="tpu_custom_call" | custom-call | tf_op jit(solution)/shard_map/lattice_step/pallas_call | solution.py:308
  11.5 0.9 %finish.1 = (f32[19,8,8,128]{3,2,1,0:T(8,128)}, f32[4,8,8,128]{3,2,1,0:T(8,128)}) custom-call(f32[19,8,8,128]{3,2,1,0:T(8,128)S(1)} %get-tuple-element.4.next_vm, f32[16,2,8,128]{3,2,1,0:T(8,128)S(1)} %get-tuple-element.5.recv_m), custom_call_target="tpu_custom_call" | custom-call | tf_op jit(solution)/shard_map/finish/pallas_call | solution.py:336

commit v2 on v1

--- a/solution.py
+++ b/solution.py
@@ -106,12 +106,13 @@
 
 
 load_chunks = ((0, 4), (4, 8))
+ack_groups = 4
 
 
 def kernel(axes, sizes, pop_hbm, out_vm, recv_m,
            pop, land_x, face_z, pack_x, pack_z, send_m,
            row_y, face_y, edge_xy, edge_yz,
-           load_sem, send_sem, recv_sem, *y_sems):
+           load_sem, send_sem, recv_sem, ack_sem, *y_sems):
     nx, ny, nz = (sizes[a] for a in axes)
     here = tuple(lax.axis_index(a) for a in axes)
     _, lx, ly, lz = pop.shape
@@ -138,9 +139,59 @@
         offsets += [(0, 1, 0), (0, -1, 0)]
         offsets += [lattice_moves[q] for q in edges_xy + edges_yz]
     partners = sorted({(a % nx, b % ny, c % nz) for a, b, c in offsets})
+    around = [o for o in partners if o[1] or o[2]]
+    me = here[0]
+    rank = (me * ny + here[1]) * nz + here[2]
+
+    def rank_of(offset):
+        a, b, c = device_at(offset)
+        return (a * ny + b) * nz + c
+
+    span = -(-nx // ack_groups)
+
+    def column(target):
+        return (target,) + here[1:]
+
     barrier = pltpu.get_barrier_semaphore()
-    for offset in partners:
-        pl.semaphore_signal(barrier, inc=1, device_id=device_at(offset), device_id_type=MESH)
+
+    def wait_some(sem, count):
+        @pl.when(count > 0)
+        def _():
+            pl.semaphore_wait(sem, count)
+
+    acks = ack_sem.at[1 + me // span]
+
+    def announce(target, carry):
+        pl.semaphore_signal(barrier, inc=1, device_id=column(target), device_id_type=MESH)
+        return carry
+
+    def acknowledge(target, carry):
+        pl.semaphore_signal(acks, inc=1, device_id=column(target), device_id_type=MESH)
+        return carry
+
+    lower = me
+    higher_z = jnp.int32(0)
+    higher_around = []
+    for offset in around:
+        @pl.when(rank_of(offset) > rank)
+        def _():
+            pl.semaphore_signal(barrier, inc=1, device_id=device_at(offset), device_id_type=MESH)
+
+        lower = lower + jnp.where(rank_of(offset) < rank, 1, 0)
+        above = jnp.where(rank_of(offset) > rank, 1, 0)
+        if offset[0] == offset[1] == 0:
+            higher_z = higher_z + above
+        else:
+            higher_around.append((device_at(offset)[0] // span, above))
+    lax.fori_loop(me + 1, nx, announce, 0)
+    wait_some(barrier, lower)
+    for offset in around:
+        @pl.when(rank_of(offset) < rank)
+        def _():
+            pl.semaphore_signal(
+                ack_sem.at[0] if offset[0] == offset[1] == 0 else acks, inc=1,
+                device_id=device_at(offset), device_id_type=MESH)
+    lax.fori_loop(0, me, acknowledge, 0)
 
     lane = lax.broadcasted_iota(jnp.int32, (ly, lz), 1)
     row = lax.broadcasted_iota(jnp.int32, (ly, lz), 0)
@@ -170,6 +221,35 @@
                 moved = rolled(value, x - z, 1) if x != z else value
                 turned[c][z] = moved if turned[c][z] is None else jnp.where(lane_x == x, moved, turned[c][z])
 
+    edge_slot = {}
+    for q in edges_xz:
+        cx, _, cz = lattice_moves[q]
+        edge_slot.setdefault((cx, cz % nz), faces + len(edge_slot))
+
+    def send_faces(chosen):
+        for sign in (1, -1):
+            @pl.when(chosen((sign, 0, 0)))
+            def _():
+                s, at = side(sign), lx - 1 if sign > 0 else 0
+                for j, q in enumerate(movers(0, sign)):
+                    remote(pop.at[q, at], land_x.at[s * faces // 2 + j], 0, (sign, 0, 0)).start()
+                for (cx, cz), slot in edge_slot.items():
+                    if cx == sign:
+                        remote(pack_x.at[s], land_x.at[slot], 0, (cx, 0, cz)).start()
+
+    def send_moments(target):
+        pltpu.make_async_remote_copy(
+            src_ref=send_m.at[target], dst_ref=recv_m.at[me],
+            send_sem=send_sem.at[2], recv_sem=recv_sem.at[2],
+            device_id=column(target), device_id_type=MESH).start()
+
+    def send_each(target, carry):
+        send_moments(target)
+        return carry
+
+    def send_z(sign):
+        remote(pack_z.at[side(sign)], face_z.at[side(sign)], 1, (0, 0, sign)).start()
+
     for i, (first, last) in enumerate(load_chunks):
         loads[i].wait()
         if i == len(load_chunks) - 1:
@@ -177,17 +257,7 @@
                 at = lx - 1 if sign > 0 else 0
                 up, down = (lattice_moves.index((sign, 0, cz)) for cz in (1, -1))
                 pack_x[side(sign)] = jnp.where(lane == lz - 1, pop[up, at], pop[down, at])
-            pl.semaphore_wait(barrier, len(partners))
-            for sign in (1, -1):
-                s, at = side(sign), lx - 1 if sign > 0 else 0
-                for j, q in enumerate(movers(0, sign)):
-                    remote(pop.at[q, at], land_x.at[s * faces // 2 + j], 0, (sign, 0, 0)).start()
-            edge_slot = {}
-            for q in edges_xz:
-                cx, _, cz = lattice_moves[q]
-                if (cx, cz % nz) not in edge_slot:
-                    edge_slot[cx, cz % nz] = faces + len(edge_slot)
-                    remote(pack_x.at[side(cx)], land_x.at[edge_slot[cx, cz % nz]], 0, lattice_moves[q]).start()
+            send_faces(lambda offset: rank_of(offset) < rank)
         for x in range(first * lx // 8, last * lx // 8):
             measure(x)
 
@@ -196,10 +266,7 @@
         for j in range(nx):
             send_m[j, p] = square[j * lx:(j + 1) * lx]
 
-    me = here[0]
-    for k in range(1, nx):
-        target = lax.rem(me + k, nx)
-        remote(send_m.at[target], recv_m.at[me], 2, (k, 0, 0)).start()
+    lax.fori_loop(0, me, send_each, 0)
 
     for sign in (1, -1):
         at = lz - 1 if sign > 0 else 0
@@ -210,23 +277,16 @@
                 packed = jnp.where(lane == k, rolled(pop[q, x], k - at, 1), packed)
         pack_z[side(sign)] = packed
     for sign in (1, -1):
-        s = side(sign)
-        remote(pack_z.at[s], face_z.at[s], 1, (0, 0, sign)).start()
-    if split_y:
-        for sign in (1, -1):
-            at = ly - 1 if sign > 0 else 0
-            for i, q in enumerate(movers(1, sign)):
-                for x in range(lx):
-                    row_y[side(sign), i, x:x + 1, :] = pop[q, x, at:at + 1, :]
-        for sign in (1, -1):
-            s = side(sign)
-            send_y(row_y.at[s], face_y.at[s], (0, sign, 0))
-        for i, q in enumerate(edges_yz):
-            s = side(lattice_moves[q][2])
-            send_y(pack_z.at[s], edge_yz.at[i], lattice_moves[q])
-        for i, q in enumerate(edges_xy):
-            s = side(lattice_moves[q][1])
-            send_y(row_y.at[s, place_in(q, 1)], edge_xy.at[i], lattice_moves[q])
+        @pl.when(rank_of((0, 0, sign)) < rank)
+        def _():
+            send_z(sign)
+
+    wait_some(ack_sem.at[0], higher_z)
+    for sign in (1, -1):
+        @pl.when(rank_of((0, 0, sign)) > rank)
+        def _():
+            send_z(sign)
+
     recv_m[me] = send_m[me]
 
     all_x = remote(land_x, land_x, 0, (1, 0, 0))
@@ -270,11 +330,43 @@
         for q in range(count_q):
             out_vm[q, x] = result[q]
 
+    def group_up(group, carry):
+        first = jnp.maximum(group * span, me + 1)
+        last = jnp.minimum(group * span + span, nx)
+        count = jnp.maximum(last - first, 0)
+        for at, above in higher_around:
+            count = count + jnp.where(at == group, above, 0)
+        wait_some(ack_sem.at[1 + group], count)
+        send_faces(lambda offset: (rank_of(offset) > rank) & (device_at(offset)[0] // span == group))
+        lax.fori_loop(first, last, send_each, 0)
+        return carry
+
+    def go_up():
+        lax.fori_loop(me // span, ack_groups, group_up, 0)
+
+    if split_y:
+        go_up()
+        for sign in (1, -1):
+            at = ly - 1 if sign > 0 else 0
+            for i, q in enumerate(movers(1, sign)):
+                for x in range(lx):
+                    row_y[side(sign), i, x:x + 1, :] = pop[q, x, at:at + 1, :]
+        for sign in (1, -1):
+            s = side(sign)
+            send_y(row_y.at[s], face_y.at[s], (0, sign, 0))
+        for i, q in enumerate(edges_yz):
+            s = side(lattice_moves[q][2])
+            send_y(pack_z.at[s], edge_yz.at[i], lattice_moves[q])
+        for i, q in enumerate(edges_xy):
+            s = side(lattice_moves[q][1])
+            send_y(row_y.at[s, place_in(q, 1)], edge_xy.at[i], lattice_moves[q])
     all_z.wait_recv()
     for copy in y_copies:
         copy.wait_recv()
     for x in range(1, lx - 1):
         advance(x)
+    if not split_y:
+        go_up()
     all_x.wait_recv()
     advance(0)
     advance(lx - 1)
@@ -327,6 +419,7 @@
             pltpu.SemaphoreType.DMA((len(load_chunks),)),
             pltpu.SemaphoreType.DMA((3,)),
             pltpu.SemaphoreType.DMA((3,)),
+            pltpu.SemaphoreType.REGULAR((1 + ack_groups,)),
         ] + y_sems,
         compiler_params=pltpu.CompilerParams(collective_id=0, has_side_effects=True),
         name="lattice_step",

time: 12.5 us -> 12.2 us (0.976)
  Pallas kernels: 11.7 us -> 11.4 us
    pallas_call x1, Pallas kernels: 10.8 us -> 10.5 us  [on_device(): pl.pallas_call(functools.partial(kernel, axes, sizes), out_shape=(pltpu.V...]
where the time goes in v2:
time: 12.2 us; the launch traced here: 12 us
  Pallas kernels  11.4 us (93%)
  between operations  0.64 us (5%)
    pallas_call x1, Pallas kernels, on_device(): pl.pallas_call(functools.partial(kernel, axes, sizes), out_shape=(pltpu.V...  10.5 us
    pallas_call x1, Pallas kernels, on_device(): pl.pallas_call(finish, out_shape=(jax.ShapeDtypeStruct(populations.shape,...  0.88 us

profile of v2, /device:TPU:0, one launch (start us, length us, event | category | flops | bytes accessed | tf_op | source)
XLA Modules:
  0.0 12.0 jit_solution(13559646464395042090)
XLA Ops:
  0.6 10.5 %lattice_step.1 = (f32[19,8,8,128]{3,2,1,0:T(8,128)S(1)}, f32[16,2,8,128]{3,2,1,0:T(8,128)S(1)}) custom-call(f32[19,8,8,128]{3,2,1,0:T(8,128)} %pop_hbm.1), custom_call_target="tpu_custom_call" | custom-call | tf_op jit(solution)/shard_map/lattice_step/pallas_call | solution.py:400
  11.1 0.9 %finish.1 = (f32[19,8,8,128]{3,2,1,0:T(8,128)}, f32[4,8,8,128]{3,2,1,0:T(8,128)}) custom-call(f32[19,8,8,128]{3,2,1,0:T(8,128)S(1)} %get-tuple-element.4.next_vm, f32[16,2,8,128]{3,2,1,0:T(8,128)S(1)} %get-tuple-element.5.recv_m), custom_call_target="tpu_custom_call" | custom-call | tf_op jit(solution)/shard_map/finish/pallas_call | solution.py:429

commit v3 on v1

v3 whole, which is shorter than its diff:
```python
import functools

import jax
import jax.numpy as jnp
from jax import lax
from jax.experimental import pallas as pl
from jax.experimental.pallas import tpu as pltpu
from jax.sharding import PartitionSpec as P

MESH = pl.DeviceIdType.MESH

lattice_moves = [
    (0, 0, 0),
    (1, 0, 0),
    (-1, 0, 0),
    (0, 1, 0),
    (0, -1, 0),
    (0, 0, 1),
    (0, 0, -1),
    (1, 1, 0),
    (-1, -1, 0),
    (1, -1, 0),
    (-1, 1, 0),
    (1, 0, 1),
    (-1, 0, -1),
    (1, 0, -1),
    (-1, 0, 1),
    (0, 1, 1),
    (0, -1, -1),
    (0, 1, -1),
    (0, -1, 1),
]
lattice_weights = [1.0 / 3.0] + [1.0 / 18.0] * 6 + [1.0 / 36.0] * 12
relaxation = 1.6
count_q = len(lattice_moves)


def movers(component, sign):
    return [q for q, move in enumerate(lattice_moves) if move[component] == sign]


def place_in(q, component):
    return movers(component, lattice_moves[q][component]).index(q)


def side(sign):
    return 0 if sign > 0 else 1


edges_xz = [q for q, m in enumerate(lattice_moves) if m[0] and m[2]]
edges_xy = [q for q, m in enumerate(lattice_moves) if m[0] and m[1]]
edges_yz = [q for q, m in enumerate(lattice_moves) if m[1] and m[2]]


def total(terms):
    terms = list(terms)
    while len(terms) > 1:
        terms = [
            terms[i] + terms[i + 1] if i + 1 < len(terms) else terms[i]
            for i in range(0, len(terms), 2)
        ]
    return terms[0]


def moments_of(f):
    density = total(f)
    inverse = 1.0 / density
    velocity = []
    for component in range(3):
        plus = total(f[q] for q in movers(component, 1))
        minus = total(f[q] for q in movers(component, -1))
        velocity.append((plus - minus) * inverse)
    return density, velocity


def collided(f):
    density, velocity = moments_of(f)
    speed_sq = velocity[0] * velocity[0] + velocity[1] * velocity[1] + velocity[2] * velocity[2]
    base = 1.0 - 1.5 * speed_sq
    scaled = {w: (relaxation * w) * density for w in set(lattice_weights)}
    keep = 1.0 - relaxation
    result = [None] * count_q
    result[0] = keep * f[0] + scaled[lattice_weights[0]] * base
    for q in range(1, count_q, 2):
        move = lattice_moves[q]
        projected = None
        for component in range(3):
            if move[component] == 0:
                continue
            if projected is None:
                projected = velocity[component] if move[component] > 0 else -velocity[component]
            elif move[component] > 0:
                projected = projected + velocity[component]
            else:
                projected = projected - velocity[component]
        even = base + 4.5 * (projected * projected)
        odd = 3.0 * projected
        weight = scaled[lattice_weights[q]]
        result[q] = keep * f[q] + weight * (even + odd)
        result[q + 1] = keep * f[q + 1] + weight * (even - odd)
    return result


def rolled(v, shift, axis):
    return pltpu.roll(v, shift % v.shape[axis], axis)


def digits(at):
    return at % 2, at // 2 % 2, at // 4


def meets(low, high, nx):
    near = high - low in (1, nx - 1)
    below = all(a <= b for a, b in zip(digits(low), digits(high)))
    return low < high and (near or below or high == nx - 1)


def load_chunks(lx):
    return ((lx // 2, lx), (0, lx // 2))


def kernel(axes, sizes, pop_hbm, out_vm, recv_m,
           pop, land_x, face_z, pack_x, pack_z, send_m,
           row_y, face_y, edge_xy, edge_yz):
    nx, ny, nz = (sizes[a] for a in axes)
    here = tuple(lax.axis_index(a) for a in axes)
    me = here[0]
    _, lx, ly, lz = pop.shape
    split_y = ny > 1
    faces = len(movers(0, 1))
    last = nx - 1
    rank = (me * ny + here[1]) * nz + here[2]
    order = sorted(range(nx), key=lambda at: (sum(digits(at)), at))

    def device_at(offset):
        return tuple(
            lax.rem(h + o % n, n) if o % n else h
            for h, o, n in zip(here, offset, (nx, ny, nz))
        )

    def rank_of(offset):
        a, b, c = device_at(offset)
        return (a * ny + b) * nz + c

    def column(target):
        return (target,) + here[1:]

    def lookup(values):
        value = jnp.int32(values[0])
        for at in range(1, nx):
            value = jnp.where(me == at, values[at], value)
        return value

    def mask(chosen):
        return lookup([sum(1 << t for t in range(nx) if chosen(at, t)) for at in range(nx)])

    offsets = [(0, 0, 1), (0, 0, -1)]
    offsets += [lattice_moves[q] for q in edges_xz]
    if split_y:
        offsets += [(0, 1, 0), (0, -1, 0)]
        offsets += [lattice_moves[q] for q in edges_xy + edges_yz]
    around = sorted({(a % nx, b % ny, c % nz) for a, b, c in offsets})

    def scoped(load_sem, send_sem, recv_sem, ack_sem, around_sem, *y_sems):
        loads = []
        for i, (first, end) in enumerate(load_chunks(lx)):
            planes = pl.ds(first, end - first)
            load = pltpu.make_async_copy(pop_hbm.at[:, planes], pop.at[:, planes], load_sem.at[i])
            load.start()
            loads.append(load)

        up = mask(lambda at, t: meets(at, t, nx))
        down = mask(lambda at, t: meets(t, at, nx))
        aside = mask(lambda at, t: at != t and not meets(at, t, nx) and not meets(t, at, nx))

        def each(chosen, targets):
            def run(body):
                for at in targets:
                    pl.when((chosen & (1 << at)) != 0)(functools.partial(body, at))
            return run

        barrier = pltpu.get_barrier_semaphore()
        lower = lookup([sum(meets(t, at, nx) for t in range(nx)) for at in range(nx)])

        @each(up, order)
        def _(at):
            pl.semaphore_signal(barrier, inc=1, device_id=column(at), device_id_type=MESH)

        for offset in around:
            @pl.when(rank_of(offset) > rank)
            def _():
                pl.semaphore_signal(barrier, inc=1, device_id=device_at(offset), device_id_type=MESH)

            lower = lower + jnp.where(rank_of(offset) < rank, 1, 0)

        @pl.when(lower > 0)
        def _():
            pl.semaphore_wait(barrier, lower)

        for offset in around:
            back = tuple(-o % n for o, n in zip(offset, (nx, ny, nz)))

            @pl.when(rank_of(offset) < rank)
            def _():
                pl.semaphore_signal(
                    around_sem.at[around.index(back)], inc=1,
                    device_id=device_at(offset), device_id_type=MESH)

        @each(down, order)
        def _(at):
            pl.semaphore_signal(ack_sem.at[me], inc=1, device_id=column(at), device_id_type=MESH)

        lane = lax.broadcasted_iota(jnp.int32, (ly, lz), 1)
        row = lax.broadcasted_iota(jnp.int32, (ly, lz), 0)

        def remote(src, dst, kind, slot, offset):
            return pltpu.make_async_remote_copy(
                src_ref=src, dst_ref=dst, send_sem=send_sem.at[kind], recv_sem=recv_sem.at[slot],
                device_id=device_at(offset), device_id_type=MESH)

        y_copies = []

        def send_y(src, dst, offset):
            i = len(y_copies)
            copy = pltpu.make_async_remote_copy(
                src_ref=src, dst_ref=dst, send_sem=y_sems[0].at[i], recv_sem=y_sems[1].at[i],
                device_id=device_at(offset), device_id_type=MESH)
            copy.start()
            y_copies.append(copy)

        edge_steps = []
        for cz in (1, -1):
            if cz % nz not in edge_steps:
                edge_steps.append(cz % nz)

        def pack_edge(sign):
            at = lx - 1 if sign > 0 else 0
            forth, back = (lattice_moves.index((sign, 0, cz)) for cz in (1, -1))
            pack_x[side(sign)] = jnp.where(lane == lz - 1, pop[forth, at], pop[back, at])

        def send_face(sign):
            s, at = side(sign), lx - 1 if sign > 0 else 0
            for j, q in enumerate(movers(0, sign)):
                remote(pop.at[q, at], land_x.at[s, j], s, s, (sign, 0, 0)).start()
            for j, cz in enumerate(edge_steps):
                remote(pack_x.at[s], land_x.at[s, faces + j], s, s, (sign, 0, cz)).start()

        def send_moments(target):
            pltpu.make_async_remote_copy(
                src_ref=send_m.at[target], dst_ref=recv_m.at[me],
                send_sem=send_sem.at[3], recv_sem=recv_sem.at[3],
                device_id=column(target), device_id_type=MESH).start()

        def send_z(sign):
            remote(pack_z.at[side(sign)], face_z.at[side(sign)], 2, 2, (0, 0, sign)).start()

        lane_x = lane & (lx - 1)
        turned = [[None] * lx for _ in range(4)]

        def measure(x):
            density, velocity = moments_of([pop[q, x] for q in range(count_q)])
            for c, value in enumerate([density] + velocity):
                for z in range(lx):
                    moved = rolled(value, x - z, 1) if x != z else value
                    held = turned[c][z]
                    turned[c][z] = moved if held is None else jnp.where(lane_x == x, moved, held)

        for i, (first, end) in enumerate(load_chunks(lx)):
            loads[i].wait()
            if first <= lx - 1 < end:
                pack_edge(1)

                @pl.when(rank_of((1, 0, 0)) < rank)
                def _():
                    send_face(1)

            for x in range(first, end):
                measure(x)

        for p in range(2):
            square = jnp.concatenate(turned[2 * p] + turned[2 * p + 1], axis=0).T
            for j in range(nx):
                send_m[j, p] = square[j * lx:(j + 1) * lx]

        each(down, order)(send_moments)

        pack_edge(-1)

        @pl.when(rank_of((-1, 0, 0)) < rank)
        def _():
            send_face(-1)

        for sign in (1, -1):
            at = lz - 1 if sign > 0 else 0
            packed = jnp.zeros((ly, lz), jnp.float32)
            for i, q in enumerate(movers(2, sign)):
                for x in range(lx):
                    k = i * lx + x
                    packed = jnp.where(lane == k, rolled(pop[q, x], k - at, 1), packed)
            pack_z[side(sign)] = packed
        for offset in around:
            if offset[0] == offset[1] == 0:
                @pl.when(rank_of(offset) > rank)
                def _():
                    pl.semaphore_wait(around_sem.at[around.index(offset)], 1)
        for sign in (1, -1):
            send_z(sign)
        recv_m[me] = send_m[me]

        all_x = [remote(land_x.at[s], land_x.at[s], s, s, (1, 0, 0)) for s in range(2)]
        all_z = remote(face_z, face_z, 2, 2, (0, 0, 1))
        others = pl.ds(0, nx - 1)
        all_m = remote(send_m.at[others], send_m.at[others], 3, 3, (1, 0, 0))

        def streamed(q, x):
            cx, cy, cz = lattice_moves[q]
            sx = x - cx
            inside = 0 <= sx < lx
            sx_wrapped = sx % lx
            v = pop[q, sx] if inside else land_x[side(cx), place_in(q, 0)]
            if cy and split_y:
                at = ly - 1 if cy > 0 else 0
                if inside:
                    other = face_y[side(cy), place_in(q, 1), sx:sx + 1, :]
                else:
                    other = edge_xy[edges_xy.index(q), sx_wrapped:sx_wrapped + 1, :]
                v = jnp.where(row == at, jnp.broadcast_to(other, v.shape), v)
            if cz:
                at = lz - 1 if cz > 0 else 0
                if inside:
                    other = face_z[side(cz)]
                    if cy and split_y:
                        at_y = ly - 1 if cy > 0 else 0
                        other = jnp.where(row == at_y, edge_yz[edges_yz.index(q)], other)
                    k = place_in(q, 2) * lx + sx
                    other = rolled(other, at - k, 1)
                else:
                    other = land_x[side(cx), faces + edge_steps.index(cz % nz)]
                v = jnp.where(lane == at, other, v)
            if cy:
                v = rolled(v, cy, 0)
            if cz:
                v = rolled(v, cz, 1)
            return v

        def advance(x):
            result = collided([streamed(q, x) for q in range(count_q)])
            for q in range(count_q):
                out_vm[q, x] = result[q]

        def go_up():
            @each(up, order)
            def _(at):
                pl.semaphore_wait(ack_sem.at[at], 1)
                if at != last:
                    send_moments(at)

            for offset in around:
                if offset[0] or offset[1]:
                    @pl.when(rank_of(offset) > rank)
                    def _():
                        pl.semaphore_wait(around_sem.at[around.index(offset)], 1)

            for sign in (-1, 1):
                @pl.when(rank_of((sign, 0, 0)) > rank)
                def _():
                    send_face(sign)

            @pl.when(me != last)
            def _():
                send_moments(last)

            each(aside, order)(send_moments)

        if split_y:
            go_up()
            for sign in (1, -1):
                at = ly - 1 if sign > 0 else 0
                for i, q in enumerate(movers(1, sign)):
                    for x in range(lx):
                        row_y[side(sign), i, x:x + 1, :] = pop[q, x, at:at + 1, :]
            for sign in (1, -1):
                send_y(row_y.at[side(sign)], face_y.at[side(sign)], (0, sign, 0))
            for i, q in enumerate(edges_yz):
                send_y(pack_z.at[side(lattice_moves[q][2])], edge_yz.at[i], lattice_moves[q])
            for i, q in enumerate(edges_xy):
                send_y(row_y.at[side(lattice_moves[q][1]), place_in(q, 1)], edge_xy.at[i], lattice_moves[q])

        all_z.wait_recv()
        for copy in y_copies:
            copy.wait_recv()
        for x in range(1, lx - 1):
            advance(x)
        if not split_y:
            go_up()
        all_x[1].wait_recv()
        advance(lx - 1)
        all_x[0].wait_recv()
        advance(0)

        for copy in all_x + [all_z, all_m] + y_copies:
            copy.wait_send()
        all_m.wait_recv()

    dma = pltpu.SemaphoreType.DMA
    y_sems = [dma((10,))] * 2 if split_y else []
    pl.run_scoped(
        scoped, dma((len(load_chunks(lx)),)), dma((4,)), dma((4,)),
        pltpu.SemaphoreType.REGULAR((nx,)), pltpu.SemaphoreType.REGULAR((len(around),)), *y_sems)


def finish(next_vm, recv_m, next_ref, slab_ref, slab_vm):
    def scoped(sems):
        store = pltpu.make_async_copy(next_vm, next_ref, sems.at[0])
        store.start()
        _, lx, ly, lz = slab_vm.shape
        for p in range(2):
            square = recv_m[:, p].reshape(lz, lz).T
            slab_vm[2 * p:2 * p + 2] = square.reshape(2, lx, ly, lz)
        slab_store = pltpu.make_async_copy(slab_vm, slab_ref, sems.at[1])
        slab_store.start()
        store.wait()
        slab_store.wait()

    pl.run_scoped(scoped, pltpu.SemaphoreType.DMA((2,)))


def on_device(axes, sizes, populations):
    q, lx, ly, lz = populations.shape
    nx, ny, nz = (sizes[a] for a in axes)
    faces = len(movers(0, 1))
    edges = 2 if nz > 2 else 1
    f32 = jnp.float32
    tile = (ly, lz)
    held = pl.pallas_call(
        functools.partial(kernel, axes, sizes),
        out_shape=(
            pltpu.VMEM(populations.shape, f32),
            pltpu.VMEM((nx, 2, lx, lz), f32),
        ),
        in_specs=[pl.BlockSpec(memory_space=pl.ANY)],
        out_specs=(pl.BlockSpec(memory_space=pltpu.VMEM),) * 2,
        scratch_shapes=[
            pltpu.VMEM(populations.shape, f32),
            pltpu.VMEM((2, faces + edges) + tile, f32),
            pltpu.VMEM((2,) + tile, f32),
            pltpu.VMEM((2,) + tile, f32),
            pltpu.VMEM((2,) + tile, f32),
            pltpu.VMEM((nx, 2, lx, lz), f32),
            pltpu.VMEM((2, 5, lx, lz), f32),
            pltpu.VMEM((2, 5, lx, lz), f32),
            pltpu.VMEM((4, lx, lz), f32),
            pltpu.VMEM((4,) + tile, f32),
        ],
        compiler_params=pltpu.CompilerParams(collective_id=0, has_side_effects=True),
        name="lattice_step",
    )(populations)
    held = [pltpu.with_memory_space_constraint(h, pltpu.VMEM) for h in held]
    slab = (4, lx, ly, lz)
    return pl.pallas_call(
        finish,
        out_shape=(jax.ShapeDtypeStruct(populations.shape, f32), jax.ShapeDtypeStruct(slab, f32)),
        in_specs=[pl.BlockSpec(memory_space=pltpu.VMEM)] * 2,
        out_specs=(pl.BlockSpec(memory_space=pl.ANY),) * 2,
        scratch_shapes=[pltpu.VMEM(slab, f32)],
        name="finish",
    )(*held)


def solution(mesh):
    axes = tuple(mesh.axis_names)
    sizes = dict(mesh.shape)
    return jax.shard_map(
        functools.partial(on_device, axes, sizes),
        mesh=mesh,
        in_specs=(P(None, "gx", "gy", "gz"),),
        out_specs=(P(None, "gx", "gy", "gz"), P(None, ("gz", "gx"), "gy", None)),
        check_vma=False,
    )
```

time: 12.5 us -> 11.9 us (0.952)
  Pallas kernels: 11.7 us -> 11 us
    pallas_call x1, Pallas kernels: 10.8 us -> 10.2 us  [on_device(): pl.pallas_call(functools.partial(kernel, axes, sizes), out_shape=(pltpu.V...]
where the time goes in v3:
time: 11.9 us; the launch traced here: 11.7 us
  Pallas kernels  11 us (92%)
  between operations  0.63 us (5%)
    pallas_call x1, Pallas kernels, on_device(): pl.pallas_call(functools.partial(kernel, axes, sizes), out_shape=(pltpu.V...  10.2 us
    pallas_call x1, Pallas kernels, on_device(): pl.pallas_call(finish, out_shape=(jax.ShapeDtypeStruct(populations.shape,...  0.86 us

profile of v3, /device:TPU:0, one launch (start us, length us, event | category | flops | bytes accessed | tf_op | source)
XLA Modules:
  0.0 11.7 jit_solution(1341273909946698937)
XLA Ops:
  0.6 10.2 %lattice_step.1 = (f32[19,8,8,128]{3,2,1,0:T(8,128)S(1)}, f32[16,2,8,128]{3,2,1,0:T(8,128)S(1)}) custom-call(f32[19,8,8,128]{3,2,1,0:T(8,128)} %pop_hbm.1), custom_call_target="tpu_custom_call" | custom-call | tf_op jit(solution)/shard_map/lattice_step/pallas_call | solution.py:435
  10.8 0.9 %finish.1 = (f32[19,8,8,128]{3,2,1,0:T(8,128)}, f32[4,8,8,128]{3,2,1,0:T(8,128)}) custom-call(f32[19,8,8,128]{3,2,1,0:T(8,128)S(1)} %get-tuple-element.4.next_vm, f32[16,2,8,128]{3,2,1,0:T(8,128)S(1)} %get-tuple-element.5.recv_m), custom_call_target="tpu_custom_call" | custom-call | tf_op jit(solution)/shard_map/finish/pallas_call | solution.py:460

commit v4 on v3

--- a/solution.py
+++ b/solution.py
@@ -109,14 +109,17 @@
     return at % 2, at // 2 % 2, at // 4
 
 
+def entry_order(nx):
+    return sorted(range(nx), key=lambda at: (sum(digits(at)), at))
+
+
 def meets(low, high, nx):
-    near = high - low in (1, nx - 1)
     below = all(a <= b for a, b in zip(digits(low), digits(high)))
-    return low < high and (near or below or high == nx - 1)
+    return low != high and (below or high == entry_order(nx)[-1]) and low != entry_order(nx)[-1]
 
 
 def load_chunks(lx):
-    return ((lx // 2, lx), (0, lx // 2))
+    return ((lx - 2, lx), (0, lx - 2))
 
 
 def kernel(axes, sizes, pop_hbm, out_vm, recv_m,
@@ -128,9 +131,8 @@
     _, lx, ly, lz = pop.shape
     split_y = ny > 1
     faces = len(movers(0, 1))
-    last = nx - 1
-    rank = (me * ny + here[1]) * nz + here[2]
-    order = sorted(range(nx), key=lambda at: (sum(digits(at)), at))
+    order = entry_order(nx)
+    last = order[-1]
 
     def device_at(offset):
         return tuple(
@@ -138,10 +140,6 @@
             for h, o, n in zip(here, offset, (nx, ny, nz))
         )
 
-    def rank_of(offset):
-        a, b, c = device_at(offset)
-        return (a * ny + b) * nz + c
-
     def column(target):
         return (target,) + here[1:]
 
@@ -150,6 +148,22 @@
         for at in range(1, nx):
             value = jnp.where(me == at, values[at], value)
         return value
+
+    def step_bits(relation):
+        return lookup([
+            relation(at, (at + 1) % nx) + 2 * relation(at, (at - 1) % nx) for at in range(nx)])
+
+    beside_lower = step_bits(lambda at, t: int(meets(t, at, nx)))
+    beside_higher = step_bits(lambda at, t: int(meets(at, t, nx) and t != last))
+
+    def beside(bits, offset):
+        return (bits & (1 if offset[0] % nx == 1 else 2)) != 0
+
+    def is_lower(offset):
+        if offset[0]:
+            return beside(beside_lower, offset)
+        _, b, c = device_at(offset)
+        return b * nz + c < here[1] * nz + here[2]
 
     def mask(chosen):
         return lookup([sum(1 << t for t in range(nx) if chosen(at, t)) for at in range(nx)])
@@ -160,6 +174,8 @@
         offsets += [(0, 1, 0), (0, -1, 0)]
         offsets += [lattice_moves[q] for q in edges_xy + edges_yz]
     around = sorted({(a % nx, b % ny, c % nz) for a, b, c in offsets})
+
+    adjacent = sorted({o[1:] for o in around if o[0]})
 
     def scoped(load_sem, send_sem, recv_sem, ack_sem, around_sem, *y_sems):
         loads = []
@@ -187,11 +203,23 @@
             pl.semaphore_signal(barrier, inc=1, device_id=column(at), device_id_type=MESH)
 
         for offset in around:
-            @pl.when(rank_of(offset) > rank)
+            goes = beside(beside_higher, offset) if offset[0] else jnp.logical_not(is_lower(offset))
+
+            @pl.when(goes)
             def _():
                 pl.semaphore_signal(barrier, inc=1, device_id=device_at(offset), device_id_type=MESH)
 
-            lower = lower + jnp.where(rank_of(offset) < rank, 1, 0)
+            comes = jnp.logical_and(is_lower(offset), me != last) if offset[0] else is_lower(offset)
+            lower = lower + jnp.where(comes, 1, 0)
+        for b, c in adjacent:
+            _, there_b, there_c = device_at((0, b, c))
+
+            @pl.when(me != last)
+            def _():
+                pl.semaphore_signal(
+                    barrier, inc=1, device_id=(last, there_b, there_c), device_id_type=MESH)
+
+        lower = lower + jnp.where(me == last, len(adjacent) * (nx - 1), 0)
 
         @pl.when(lower > 0)
         def _():
@@ -200,7 +228,7 @@
         for offset in around:
             back = tuple(-o % n for o, n in zip(offset, (nx, ny, nz)))
 
-            @pl.when(rank_of(offset) < rank)
+            @pl.when(me == last if offset[0] else is_lower(offset))
             def _():
                 pl.semaphore_signal(
                     around_sem.at[around.index(back)], inc=1,
@@ -270,7 +298,7 @@
             if first <= lx - 1 < end:
                 pack_edge(1)
 
-                @pl.when(rank_of((1, 0, 0)) < rank)
+                @pl.when(is_lower((1, 0, 0)))
                 def _():
                     send_face(1)
 
@@ -282,11 +310,11 @@
             for j in range(nx):
                 send_m[j, p] = square[j * lx:(j + 1) * lx]
 
-        each(down, order)(send_moments)
+        each(down, order[:5])(send_moments)
 
         pack_edge(-1)
 
-        @pl.when(rank_of((-1, 0, 0)) < rank)
+        @pl.when(is_lower((-1, 0, 0)))
         def _():
             send_face(-1)
 
@@ -300,11 +328,12 @@
             pack_z[side(sign)] = packed
         for offset in around:
             if offset[0] == offset[1] == 0:
-                @pl.when(rank_of(offset) > rank)
+                @pl.when(jnp.logical_not(is_lower(offset)))
                 def _():
                     pl.semaphore_wait(around_sem.at[around.index(offset)], 1)
         for sign in (1, -1):
             send_z(sign)
+        each(down, order[5:])(send_moments)
         recv_m[me] = send_m[me]
 
         all_x = [remote(land_x.at[s], land_x.at[s], s, s, (1, 0, 0)) for s in range(2)]
@@ -357,12 +386,12 @@
 
             for offset in around:
                 if offset[0] or offset[1]:
-                    @pl.when(rank_of(offset) > rank)
+                    @pl.when(me == (last - offset[0]) % nx if offset[0] else jnp.logical_not(is_lower(offset)))
                     def _():
                         pl.semaphore_wait(around_sem.at[around.index(offset)], 1)
 
             for sign in (-1, 1):
-                @pl.when(rank_of((sign, 0, 0)) > rank)
+                @pl.when(jnp.logical_not(is_lower((sign, 0, 0))))
                 def _():
                     send_face(sign)
 
@@ -372,8 +401,8 @@
 
             each(aside, order)(send_moments)
 
+        go_up()
         if split_y:
-            go_up()
             for sign in (1, -1):
                 at = ly - 1 if sign > 0 else 0
                 for i, q in enumerate(movers(1, sign)):
@@ -391,8 +420,6 @@
             copy.wait_recv()
         for x in range(1, lx - 1):
             advance(x)
-        if not split_y:
-            go_up()
         all_x[1].wait_recv()
         advance(lx - 1)
         all_x[0].wait_recv()

time: 11.9 us -> 11.8 us (level)
  no operation moved by 1% of the time
where the time goes in v4:
time: 11.8 us; the launch traced here: 11.6 us
  Pallas kernels  11 us (93%)
  between operations  0.63 us (5%)
    pallas_call x1, Pallas kernels, on_device(): pl.pallas_call(functools.partial(kernel, axes, sizes), out_shape=(pltpu.V...  10.1 us
    pallas_call x1, Pallas kernels, on_device(): pl.pallas_call(finish, out_shape=(jax.ShapeDtypeStruct(populations.shape,...  0.86 us

profile of v4, /device:TPU:0, one launch (start us, length us, event | category | flops | bytes accessed | tf_op | source)
XLA Modules:
  0.0 11.6 jit_solution(4882303910745232148)
XLA Ops:
  0.6 10.1 %lattice_step.1 = (f32[19,8,8,128]{3,2,1,0:T(8,128)S(1)}, f32[16,2,8,128]{3,2,1,0:T(8,128)S(1)}) custom-call(f32[19,8,8,128]{3,2,1,0:T(8,128)} %pop_hbm.1), custom_call_target="tpu_custom_call" | custom-call | tf_op jit(solution)/shard_map/lattice_step/pallas_call | solution.py:462
  10.8 0.9 %finish.1 = (f32[19,8,8,128]{3,2,1,0:T(8,128)}, f32[4,8,8,128]{3,2,1,0:T(8,128)}) custom-call(f32[19,8,8,128]{3,2,1,0:T(8,128)S(1)} %get-tuple-element.4.next_vm, f32[16,2,8,128]{3,2,1,0:T(8,128)S(1)} %get-tuple-element.5.recv_m), custom_call_target="tpu_custom_call" | custom-call | tf_op jit(solution)/shard_map/finish/pallas_call | solution.py:487

commit v5 on v4

--- a/solution.py
+++ b/solution.py
@@ -119,11 +119,11 @@
 
 
 def load_chunks(lx):
-    return ((lx - 2, lx), (0, lx - 2))
+    return ((lx - 1, lx), (0, lx - 1))
 
 
 def kernel(axes, sizes, pop_hbm, out_vm, recv_m,
-           pop, land_x, face_z, pack_x, pack_z, send_m,
+           pop, land_x, face_z, turned, pack_x, pack_z, send_m,
            row_y, face_y, edge_xy, edge_yz):
     nx, ny, nz = (sizes[a] for a in axes)
     here = tuple(lax.axis_index(a) for a in axes)
@@ -262,16 +262,29 @@
                 edge_steps.append(cz % nz)
 
         def pack_edge(sign):
-            at = lx - 1 if sign > 0 else 0
-            forth, back = (lattice_moves.index((sign, 0, cz)) for cz in (1, -1))
-            pack_x[side(sign)] = jnp.where(lane == lz - 1, pop[forth, at], pop[back, at])
-
-        def send_face(sign):
+            s, at = side(sign), lx - 1 if sign > 0 else 0
+            for j, cz in enumerate((1, -1)):
+                turned[s, j] = rolled(pop[lattice_moves.index((sign, 0, cz)), at], cz, 1)
+            pack_x[s] = jnp.where(lane == 0, turned[s, 0], turned[s, 1])
+
+        def send_plain(sign):
             s, at = side(sign), lx - 1 if sign > 0 else 0
             for j, q in enumerate(movers(0, sign)):
-                remote(pop.at[q, at], land_x.at[s, j], s, s, (sign, 0, 0)).start()
+                if not lattice_moves[q][2]:
+                    remote(pop.at[q, at], land_x.at[s, j], s, s, (sign, 0, 0)).start()
+
+        def send_turned(sign):
+            s = side(sign)
+            for j, q in enumerate(movers(0, sign)):
+                if lattice_moves[q][2]:
+                    i = (1, -1).index(lattice_moves[q][2])
+                    remote(turned.at[s, i], land_x.at[s, j], s, s, (sign, 0, 0)).start()
             for j, cz in enumerate(edge_steps):
                 remote(pack_x.at[s], land_x.at[s, faces + j], s, s, (sign, 0, cz)).start()
+
+        def send_face(sign):
+            send_plain(sign)
+            send_turned(sign)
 
         def send_moments(target):
             pltpu.make_async_remote_copy(
@@ -283,34 +296,54 @@
             remote(pack_z.at[side(sign)], face_z.at[side(sign)], 2, 2, (0, 0, sign)).start()
 
         lane_x = lane & (lx - 1)
-        turned = [[None] * lx for _ in range(4)]
+        values = [[None] * lx for _ in range(4)]
 
         def measure(x):
             density, velocity = moments_of([pop[q, x] for q in range(count_q)])
             for c, value in enumerate([density] + velocity):
-                for z in range(lx):
-                    moved = rolled(value, x - z, 1) if x != z else value
-                    held = turned[c][z]
-                    turned[c][z] = moved if held is None else jnp.where(lane_x == x, moved, held)
+                values[c][x] = value
+
+        def skewed(tiles):
+            step = 1
+            while step < lx:
+                odd = (lane & step) != 0
+                tiles = [jnp.where(odd, tiles[(k + step) % lx], tiles[k]) for k in range(lx)]
+                step *= 2
+            return tiles
+
+        def exchanged(tiles):
+            tiles = skewed(tiles)
+            tiles = [tiles[0]] + [
+                jnp.where(lane_x >= k, rolled(tiles[k], k, 1), rolled(tiles[k], k - lx, 1))
+                for k in range(1, lx)]
+            tiles = skewed(tiles)
+            return [tiles[-z % lx] for z in range(lx)]
 
         for i, (first, end) in enumerate(load_chunks(lx)):
             loads[i].wait()
             if first <= lx - 1 < end:
-                pack_edge(1)
-
                 @pl.when(is_lower((1, 0, 0)))
                 def _():
-                    send_face(1)
+                    send_plain(1)
+
+                pack_edge(1)
+
+                @pl.when(is_lower((1, 0, 0)))
+                def _():
+                    send_turned(1)
 
             for x in range(first, end):
                 measure(x)
 
         for p in range(2):
-            square = jnp.concatenate(turned[2 * p] + turned[2 * p + 1], axis=0).T
+            rows = exchanged(values[2 * p]) + exchanged(values[2 * p + 1])
+            square = jnp.concatenate(rows, axis=0).T
             for j in range(nx):
                 send_m[j, p] = square[j * lx:(j + 1) * lx]
 
-        each(down, order[:5])(send_moments)
+        early = jnp.where(here[2] == 0, down, 0)
+        each(down, order[:1])(send_moments)
+        each(early, order[1:1])(send_moments)
 
         pack_edge(-1)
 
@@ -333,7 +366,7 @@
                     pl.semaphore_wait(around_sem.at[around.index(offset)], 1)
         for sign in (1, -1):
             send_z(sign)
-        each(down, order[5:])(send_moments)
+        each(early, order[1:])(send_moments)
         recv_m[me] = send_m[me]
 
         all_x = [remote(land_x.at[s], land_x.at[s], s, s, (1, 0, 0)) for s in range(2)]
@@ -365,6 +398,7 @@
                     other = rolled(other, at - k, 1)
                 else:
                     other = land_x[side(cx), faces + edge_steps.index(cz % nz)]
+                    return jnp.where(lane == lz - 1 - at, other, v)
                 v = jnp.where(lane == at, other, v)
             if cy:
                 v = rolled(v, cy, 0)
@@ -372,8 +406,13 @@
                 v = rolled(v, cz, 1)
             return v
 
-        def advance(x):
-            result = collided([streamed(q, x) for q in range(count_q)])
+        def gather(x, known):
+            return {q: streamed(q, x) for q in range(count_q) if (0 <= x - lattice_moves[q][0] < lx) == known}
+
+        def advance(x, known=None):
+            f = dict(known or gather(x, True))
+            f.update(gather(x, False))
+            result = collided([f[q] for q in range(count_q)])
             for q in range(count_q):
                 out_vm[q, x] = result[q]
 
@@ -420,10 +459,13 @@
             copy.wait_recv()
         for x in range(1, lx - 1):
             advance(x)
+        each(down - early, order[1:])(send_moments)
+        known = gather(lx - 1, True)
         all_x[1].wait_recv()
-        advance(lx - 1)
+        advance(lx - 1, known)
+        known = gather(0, True)
         all_x[0].wait_recv()
-        advance(0)
+        advance(0, known)
 
         for copy in all_x + [all_z, all_m] + y_copies:
             copy.wait_send()
@@ -471,6 +513,7 @@
             pltpu.VMEM(populations.shape, f32),
             pltpu.VMEM((2, faces + edges) + tile, f32),
             pltpu.VMEM((2,) + tile, f32),
+            pltpu.VMEM((2, 2) + tile, f32),
             pltpu.VMEM((2,) + tile, f32),
             pltpu.VMEM((2,) + tile, f32),
             pltpu.VMEM((nx, 2, lx, lz), f32),

time: 11.8 us -> 11.6 us (0.983)
  Pallas kernels: 11 us -> 10.8 us
    pallas_call x1, Pallas kernels: 10.1 us -> 9.96 us  [on_device(): pl.pallas_call(functools.partial(kernel, axes, sizes), out_shape=(pltpu.V...]
where the time goes in v5:
time: 11.6 us; the launch traced here: 11.4 us
  Pallas kernels  10.8 us (93%)
  between operations  0.63 us (5%)
    pallas_call x1, Pallas kernels, on_device(): pl.pallas_call(functools.partial(kernel, axes, sizes), out_shape=(pltpu.V...  9.96 us
    pallas_call x1, Pallas kernels, on_device(): pl.pallas_call(finish, out_shape=(jax.ShapeDtypeStruct(populations.shape,...  0.86 us

profile of v5, /device:TPU:0, one launch (start us, length us, event | category | flops | bytes accessed | tf_op | source)
XLA Modules:
  0.0 11.4 jit_solution(3323741745484441936)
XLA Ops:
  0.6 10.0 %lattice_step.1 = (f32[19,8,8,128]{3,2,1,0:T(8,128)S(1)}, f32[16,2,8,128]{3,2,1,0:T(8,128)S(1)}) custom-call(f32[19,8,8,128]{3,2,1,0:T(8,128)} %pop_hbm.1), custom_call_target="tpu_custom_call" | custom-call | tf_op jit(solution)/shard_map/lattice_step/pallas_call | solution.py:504
  10.6 0.9 %finish.1 = (f32[19,8,8,128]{3,2,1,0:T(8,128)}, f32[4,8,8,128]{3,2,1,0:T(8,128)}) custom-call(f32[19,8,8,128]{3,2,1,0:T(8,128)S(1)} %get-tuple-element.4.next_vm, f32[16,2,8,128]{3,2,1,0:T(8,128)S(1)} %get-tuple-element.5.recv_m), custom_call_target="tpu_custom_call" | custom-call | tf_op jit(solution)/shard_map/finish/pallas_call | solution.py:530

commit v6 on v5

--- a/solution.py
+++ b/solution.py
@@ -429,6 +429,8 @@
                     def _():
                         pl.semaphore_wait(around_sem.at[around.index(offset)], 1)
 
+            each(aside, (order[4],))(send_moments)
+
             for sign in (-1, 1):
                 @pl.when(jnp.logical_not(is_lower((sign, 0, 0))))
                 def _():
@@ -438,7 +440,7 @@
             def _():
                 send_moments(last)
 
-            each(aside, order)(send_moments)
+            each(aside, [at for at in order if at not in (order[4],)])(send_moments)
 
         go_up()
         if split_y:

time: 11.6 us -> 11.6 us (level)
  no operation moved by 1% of the time
where the time goes in v6:
time: 11.6 us; the launch traced here: 11.4 us
  Pallas kernels  10.8 us (93%)
  between operations  0.63 us (5%)
    pallas_call x1, Pallas kernels, on_device(): pl.pallas_call(functools.partial(kernel, axes, sizes), out_shape=(pltpu.V...  9.96 us
    pallas_call x1, Pallas kernels, on_device(): pl.pallas_call(finish, out_shape=(jax.ShapeDtypeStruct(populations.shape,...  0.86 us

profile of v6, /device:TPU:0, one launch (start us, length us, event | category | flops | bytes accessed | tf_op | source)
XLA Modules:
  0.0 11.4 jit_solution(15006645201408706881)
XLA Ops:
  0.6 10.0 %lattice_step.1 = (f32[19,8,8,128]{3,2,1,0:T(8,128)S(1)}, f32[16,2,8,128]{3,2,1,0:T(8,128)S(1)}) custom-call(f32[19,8,8,128]{3,2,1,0:T(8,128)} %pop_hbm.1), custom_call_target="tpu_custom_call" | custom-call | tf_op jit(solution)/shard_map/lattice_step/pallas_call | solution.py:506
  10.6 0.9 %finish.1 = (f32[19,8,8,128]{3,2,1,0:T(8,128)}, f32[4,8,8,128]{3,2,1,0:T(8,128)}) custom-call(f32[19,8,8,128]{3,2,1,0:T(8,128)S(1)} %get-tuple-element.4.next_vm, f32[16,2,8,128]{3,2,1,0:T(8,128)S(1)} %get-tuple-element.5.recv_m), custom_call_target="tpu_custom_call" | custom-call | tf_op jit(solution)/shard_map/finish/pallas_call | solution.py:532

commit v7 on v6

--- a/solution.py
+++ b/solution.py
@@ -198,19 +198,6 @@
         barrier = pltpu.get_barrier_semaphore()
         lower = lookup([sum(meets(t, at, nx) for t in range(nx)) for at in range(nx)])
 
-        @each(up, order)
-        def _(at):
-            pl.semaphore_signal(barrier, inc=1, device_id=column(at), device_id_type=MESH)
-
-        for offset in around:
-            goes = beside(beside_higher, offset) if offset[0] else jnp.logical_not(is_lower(offset))
-
-            @pl.when(goes)
-            def _():
-                pl.semaphore_signal(barrier, inc=1, device_id=device_at(offset), device_id_type=MESH)
-
-            comes = jnp.logical_and(is_lower(offset), me != last) if offset[0] else is_lower(offset)
-            lower = lower + jnp.where(comes, 1, 0)
         for b, c in adjacent:
             _, there_b, there_c = device_at((0, b, c))
 
@@ -219,6 +206,19 @@
                 pl.semaphore_signal(
                     barrier, inc=1, device_id=(last, there_b, there_c), device_id_type=MESH)
 
+        @each(up, order[::-1])
+        def _(at):
+            pl.semaphore_signal(barrier, inc=1, device_id=column(at), device_id_type=MESH)
+
+        for offset in around:
+            goes = beside(beside_higher, offset) if offset[0] else jnp.logical_not(is_lower(offset))
+
+            @pl.when(goes)
+            def _():
+                pl.semaphore_signal(barrier, inc=1, device_id=device_at(offset), device_id_type=MESH)
+
+            comes = jnp.logical_and(is_lower(offset), me != last) if offset[0] else is_lower(offset)
+            lower = lower + jnp.where(comes, 1, 0)
         lower = lower + jnp.where(me == last, len(adjacent) * (nx - 1), 0)
 
         @pl.when(lower > 0)
@@ -295,7 +295,7 @@
         def send_z(sign):
             remote(pack_z.at[side(sign)], face_z.at[side(sign)], 2, 2, (0, 0, sign)).start()
 
-        lane_x = lane & (lx - 1)
+        over = row < (lane // ly) % lx
         values = [[None] * lx for _ in range(4)]
 
         def measure(x):
@@ -313,9 +313,7 @@
 
         def exchanged(tiles):
             tiles = skewed(tiles)
-            tiles = [tiles[0]] + [
-                jnp.where(lane_x >= k, rolled(tiles[k], k, 1), rolled(tiles[k], k - lx, 1))
-                for k in range(1, lx)]
+            tiles = [rolled(tiles[k], k, 1) if k else tiles[k] for k in range(lx)]
             tiles = skewed(tiles)
             return [tiles[-z % lx] for z in range(lx)]
 
@@ -335,11 +333,12 @@
             for x in range(first, end):
                 measure(x)
 
+        rows = [exchanged(values[c]) for c in range(4)]
         for p in range(2):
-            rows = exchanged(values[2 * p]) + exchanged(values[2 * p + 1])
-            square = jnp.concatenate(rows, axis=0).T
+            square = jnp.concatenate(rows[2 * p] + rows[2 * p + 1], axis=0).T
+            pieces = [square[j * lx:(j + 1) * lx] for j in range(nx)]
             for j in range(nx):
-                send_m[j, p] = square[j * lx:(j + 1) * lx]
+                send_m[j, p] = jnp.where(over, pieces[(j + 1) % nx], pieces[j])
 
         early = jnp.where(here[2] == 0, down, 0)
         each(down, order[:1])(send_moments)

time: 11.6 us -> 11.6 us (level)
  no operation moved by 1% of the time
where the time goes in v7:
time: 11.6 us; the launch traced here: 11.4 us
  Pallas kernels  10.8 us (93%)
  between operations  0.63 us (5%)
    pallas_call x1, Pallas kernels, on_device(): pl.pallas_call(functools.partial(kernel, axes, sizes), out_shape=(pltpu.V...  9.94 us
    pallas_call x1, Pallas kernels, on_device(): pl.pallas_call(finish, out_shape=(jax.ShapeDtypeStruct(populations.shape,...  0.86 us

profile of v7, /device:TPU:0, one launch (start us, length us, event | category | flops | bytes accessed | tf_op | source)
XLA Modules:
  0.0 11.4 jit_solution(1514319250052280645)
XLA Ops:
  0.6 9.9 %lattice_step.1 = (f32[19,8,8,128]{3,2,1,0:T(8,128)S(1)}, f32[16,2,8,128]{3,2,1,0:T(8,128)S(1)}) custom-call(f32[19,8,8,128]{3,2,1,0:T(8,128)} %pop_hbm.1), custom_call_target="tpu_custom_call" | custom-call | tf_op jit(solution)/shard_map/lattice_step/pallas_call | solution.py:505
  10.6 0.9 %finish.1 = (f32[19,8,8,128]{3,2,1,0:T(8,128)}, f32[4,8,8,128]{3,2,1,0:T(8,128)}) custom-call(f32[19,8,8,128]{3,2,1,0:T(8,128)S(1)} %get-tuple-element.4.next_vm, f32[16,2,8,128]{3,2,1,0:T(8,128)S(1)} %get-tuple-element.5.recv_m), custom_call_target="tpu_custom_call" | custom-call | tf_op jit(solution)/shard_map/finish/pallas_call | solution.py:531

commit v8 on v7

--- a/solution.py
+++ b/solution.py
@@ -320,13 +320,13 @@
         for i, (first, end) in enumerate(load_chunks(lx)):
             loads[i].wait()
             if first <= lx - 1 < end:
-                @pl.when(is_lower((1, 0, 0)))
+                @pl.when(is_lower((1, 0, 0)) & (here[2] == 0))
                 def _():
                     send_plain(1)
 
                 pack_edge(1)
 
-                @pl.when(is_lower((1, 0, 0)))
+                @pl.when(is_lower((1, 0, 0)) & (here[2] == 0))
                 def _():
                     send_turned(1)
 
@@ -342,6 +342,11 @@
 
         early = jnp.where(here[2] == 0, down, 0)
         each(down, order[:1])(send_moments)
+
+        @pl.when(is_lower((1, 0, 0)) & (here[2] != 0))
+        def _():
+            send_face(1)
+
         each(early, order[1:1])(send_moments)
 
         pack_edge(-1)
@@ -428,7 +433,7 @@
                     def _():
                         pl.semaphore_wait(around_sem.at[around.index(offset)], 1)
 
-            each(aside, (order[4],))(send_moments)
+            each(aside, order[4:5])(send_moments)
 
             for sign in (-1, 1):
                 @pl.when(jnp.logical_not(is_lower((sign, 0, 0))))
@@ -439,7 +444,7 @@
             def _():
                 send_moments(last)
 
-            each(aside, [at for at in order if at not in (order[4],)])(send_moments)
+            each(aside, [at for at in order if at not in order[4:5]])(send_moments)
 
         go_up()
         if split_y:

time: 11.6 us -> 11.6 us (level)
  no operation moved by 1% of the time
where the time goes in v8:
time: 11.6 us; the launch traced here: 11.4 us
  Pallas kernels  10.8 us (93%)
  between operations  0.63 us (5%)
    pallas_call x1, Pallas kernels, on_device(): pl.pallas_call(functools.partial(kernel, axes, sizes), out_shape=(pltpu.V...  9.95 us
    pallas_call x1, Pallas kernels, on_device(): pl.pallas_call(finish, out_shape=(jax.ShapeDtypeStruct(populations.shape,...  0.86 us

profile of v8, /device:TPU:0, one launch (start us, length us, event | category | flops | bytes accessed | tf_op | source)
XLA Modules:
  0.0 11.4 jit_solution(15535514678242417810)
XLA Ops:
  0.6 9.9 %lattice_step.1 = (f32[19,8,8,128]{3,2,1,0:T(8,128)S(1)}, f32[16,2,8,128]{3,2,1,0:T(8,128)S(1)}) custom-call(f32[19,8,8,128]{3,2,1,0:T(8,128)} %pop_hbm.1), custom_call_target="tpu_custom_call" | custom-call | tf_op jit(solution)/shard_map/lattice_step/pallas_call | solution.py:510
  10.6 0.9 %finish.1 = (f32[19,8,8,128]{3,2,1,0:T(8,128)}, f32[4,8,8,128]{3,2,1,0:T(8,128)}) custom-call(f32[19,8,8,128]{3,2,1,0:T(8,128)S(1)} %get-tuple-element.4.next_vm, f32[16,2,8,128]{3,2,1,0:T(8,128)S(1)} %get-tuple-element.5.recv_m), custom_call_target="tpu_custom_call" | custom-call | tf_op jit(solution)/shard_map/finish/pallas_call | solution.py:536
